TPU v7x, 32 devices: a whole 2x2x4 slice. The times are simulated.
32 devices in a mesh: row: 4 (over y, x), col: 4 (over z), depth: 2 (over core).
Axes of the slice: x: 2, y: 2, z: 4, core: 2. Of those that a mesh axis runs over, the one named last changes fastest.
Arguments:
- orbitals: bfloat16 [2, 1024, 2, 4096], P(None, ('row', 'col'), 'depth'), may hold values from -20 to 20
- potential: float32 [2, 4096], P('depth'), may hold values from -6 to 6
Outputs:
- intersection: float32 [1024, 2, 1024], P(('row', 'depth'), None, 'col')
- applied: bfloat16 [2, 1024, 2, 4096], P(None, ('row', 'col'), 'depth')
All inputs are finite; a program needn't handle non-finite values.
Results may differ from a plain program's by a relative error of at most 0.001.
Values may be sent and summed in bfloat16 or wider, within the bound.
A program may use at most 128 MiB of HBM per device.

v0:
```python
import jax
import jax.numpy as jnp
from jax import lax
from jax.sharding import PartitionSpec as P

NX = 64


def with_halo(block, sides, width):
    for axis, dim in sides:
        count = lax.axis_size(axis)
        forward = [(i, i + 1) for i in range(count - 1)]
        forward.append((count - 1, 0))
        backward = [(target, source) for source, target in forward]
        low = lax.ppermute(
            lax.slice_in_dim(block, block.shape[dim] - width, None, axis=dim), axis, forward
        )
        high = lax.ppermute(lax.slice_in_dim(block, 0, width, axis=dim), axis, backward)
        block = jnp.concatenate([low, block, high], axis=dim)
    return block


def apply_operator(padded, potential):
    center = padded[:, :, 1:-1].astype(jnp.float32)
    below = padded[:, :, :-2].astype(jnp.float32)
    above = padded[:, :, 2:].astype(jnp.float32)
    flat_cells = center.shape[-1]
    xpos = jnp.arange(flat_cells) % NX
    yminus = jnp.roll(center, NX, axis=3)
    yplus = jnp.roll(center, -NX, axis=3)
    xminus = jnp.where(xpos == 0, jnp.roll(center, 1 - NX, axis=3), jnp.roll(center, 1, axis=3))
    xplus = jnp.where(
        xpos == NX - 1, jnp.roll(center, NX - 1, axis=3), jnp.roll(center, -1, axis=3)
    )
    lap = below + above + yminus + yplus + xminus + xplus - 6.0 * center
    return (-0.5 * lap + potential[None, None] * center).astype(jnp.bfloat16)


def contract(left, right):
    return lax.dot_general(
        left, right, (((1,), (1,)), ((), ())), preferred_element_type=jnp.float32
    )


def shards(orbitals, potential):
    parts, orbs, planes, cells = orbitals.shape
    flat = orbitals.reshape(parts, orbs, planes * cells)
    panel = lax.all_gather(flat, "col", axis=1, tiled=True)
    other = lax.all_gather(flat, "row", axis=1, tiled=True)
    padded = with_halo(orbitals, (("depth", 2),), 1)
    applied = apply_operator(padded, potential)
    dvol = 1.0 / (planes * lax.axis_size("depth") * cells)
    tile_cols = other.shape[1]
    real_rows = panel[0]
    imag_rows = panel[1]
    sreal = contract(real_rows, other[0]) + contract(imag_rows, other[1])
    simag = contract(real_rows, other[1]) - contract(imag_rows, other[0])
    summed = lax.psum_scatter(
        dvol * jnp.concatenate([sreal, simag], axis=1), "depth", scatter_dimension=0, tiled=True
    )
    intersection = summed.reshape(summed.shape[0], 2, tile_cols)
    intersection = lax.all_to_all(intersection, "col", split_axis=2, concat_axis=2, tiled=True)
    return (intersection, applied)


def solution(mesh):
    in_specs = (P(None, ("row", "col"), "depth", None), P("depth", None))
    out_specs = (P(("row", "depth"), None, "col"), P(None, ("row", "col"), "depth", None))
    return jax.shard_map(shards, mesh=mesh, in_specs=in_specs, out_specs=out_specs, check_vma=False)
```

profile of v0, /device:TPU:0, one launch (start us, length us, event | category | flops | bytes accessed | tf_op | source)
XLA Modules:
  0.0 186.1 jit_solution(16060242905263434024)
XLA Ops:
  7.2 0.0 copy-start
  7.2 0.0 all-gather.7.cloned.1.call-start
  7.2 0.7 all-gather.7.cloned.1.call-update
  7.9 0.0 all-gather.5.cloned.1.call-start
  8.0 0.7 all-gather.5.cloned.1.call-update
  8.7 0.0 reduce-scatter.2.cloned.1.call-start
  8.7 0.0 copy-done
  8.7 0.6 collective-permute-start
  9.3 0.1 collective-permute-start.1
  9.4 0.1 fusion.23
  9.4 0.7 fusion.20
  10.1 0.7 fusion.19
  10.8 1.8 fusion.21
  12.7 2.4 %fusion.22 = (f32[2,64,1,4032]{3,1,2,0:T(8,128)}, f32[2,64,1,4032]{3,1,2,0:T(8,128)}) fusion(bf16[2,64,1,4096]{3,1,2,0:T(8,128)(2,1)S(1)} %copy-done), kind=kLoop, calls=%fused_computation.32 | loop fusion | bytes 8257536 | tf_op jit(solution)/shard_map/jit(_roll_static)/slice | solution.py:30
  15.1 50.1 %all-gather.7.cloned.1.call-done = bf16[2,256,1,4096]{3,1,2,0:T(8,128)(2,1)} async-done(((bf16[2,64,1,4096]{3,1,2,0:T(8,128)(2,1)}), bf16[2,256,1,4096]{3,1,2,0:T(8,128)(2,1)}) %all-gather.7.cloned.1.call-update) | async-done | bytes 4194320 | tf_op jit(solution)/shard_map/all_gather | solution.py:49
  65.2 82.3 %all-gather.5.cloned.1.call-done = bf16[2,256,1,4096]{3,1,2,0:T(8,128)(2,1)} async-done(((bf16[2,64,1,4096]{3,1,2,0:T(8,128)(2,1)}), bf16[2,256,1,4096]{3,1,2,0:T(8,128)(2,1)}) %all-gather.5.cloned.1.call-update) | async-done | bytes 4194320 | tf_op jit(solution)/shard_map/all_gather | solution.py:48
  147.5 0.0 copy-start.2
  147.5 3.1 %fusion.7 = f32[256,256]{0,1:T(8,128)S(1)} fusion(bf16[2,256,1,4096]{3,1,2,0:T(8,128)(2,1)} %all-gather.5.cloned.1.call-done, bf16[2,256,1,4096]{3,1,2,0:T(8,128)(2,1)} %all-gather.7.cloned.1.call-done), kind=kOutput, calls=%fused_computation.14 | convolution fusion | flops 536870912 | bytes 4456448 | tf_op jit(solution)/shard_map/dot_general | solution.py:40
  150.6 0.3 copy-done.2
  150.9 0.0 copy-start.3
  150.9 2.5 %fusion.8 = f32[256,256]{0,1:T(8,128)S(1)} fusion(bf16[2,256,1,4096]{3,1,2,0:T(8,128)(2,1)} %all-gather.5.cloned.1.call-done, bf16[2,256,1,4096]{3,1,2,0:T(8,128)(2,1)S(1)} %copy-done.2), kind=kOutput, calls=%fused_computation.15 | convolution fusion | flops 536870912 | bytes 4456448 | tf_op jit(solution)/shard_map/dot_general | solution.py:40
  153.4 0.3 copy-done.3
  153.8 0.7 fusion.12
  154.5 0.7 fusion.11
  155.3 0.8 maximum_multiply_fusion
  156.1 0.0 reduce-scatter.2.cloned.1.call-update
  156.1 0.6 fusion.15
  156.7 0.0 copy-start.1
  156.7 2.4 %fusion.18 = (f32[2,64,1,4095]{3,1,2,0:T(8,128)}, f32[2,64,1,4095]{3,1,2,0:T(8,128)}) fusion(bf16[2,64,1,4096]{3,1,2,0:T(8,128)(2,1)S(1)} %copy-done), kind=kLoop, calls=%fused_computation.28 | loop fusion | bytes 8386560 | tf_op jit(solution)/shard_map/jit(_roll_static)/slice | solution.py:33
  159.1 3.5 %reduce-scatter.2.cloned.1.call-done = f32[128,512]{0,1:T(8,128)} async-done(((f32[256,512]{0,1:T(8,128)}), f32[128,512]{0,1:T(8,128)}) %reduce-scatter.2.cloned.1.call-update) | async-done | bytes 262160 | tf_op jit(solution)/shard_map/reduce_scatter | solution.py:58
  162.7 1.9 copy.7
  164.5 4.8 %all-to-all-start = ((f32[128,2,256]{0,1,2:T(2,128)}), f32[128,2,256]{0,1,2:T(2,128)S(1)}, u32[]{:S(2)}, u32[]{:S(2)}) async-start(f32[128,2,256]{0,1,2:T(2,128)} %copy.7), calls=%async_computation.1 | async-start | bytes 524288 | tf_op jit(solution)/shard_map/all_to_all | solution.py:62
  169.3 0.0 collective-permute-done
  169.3 0.0 collective-permute-done.1
  169.3 0.0 copy-done.1
  169.3 6.8 %fusion.6 = bf16[2,64,1,4096]{3,1,2,0:T(8,128)(2,1)} fusion(f32[2,64,1,4032]{3,1,2,0:T(8,128)} %get-tuple-element.15, f32[2,64,1,64]{3,1,2,0:T(8,128)S(1)} %get-tuple-element.17, f32[2,64,1,64]{3,1,2,0:T(8,128)S(1)} %get-tuple-element.16, f32[2,64,1,4032]{3,1,2,0:T(8,128)} %get-tuple-element.14, f32[2,64,1,63]{3,1,2,0:T(8,128)} %get-tuple-element.11, ...), kind=kLoop, calls=%fused_computation.11 | loop fusion | flops 11534336 | bytes 16801792 | tf_op jit(solution)/shard_map/convert_element_type | solution.py:36
  176.2 2.6 %all-to-all-done = f32[128,2,256]{0,1,2:T(2,128)S(1)} async-done(((f32[128,2,256]{0,1,2:T(2,128)}), f32[128,2,256]{0,1,2:T(2,128)S(1)}, u32[]{:S(2)}, u32[]{:S(2)}) %all-to-all-start) | async-done | bytes 262176 | tf_op jit(solution)/shard_map/all_to_all | solution.py:62
  178.7 0.8 copy.8
Async XLA Ops:
  7.2 1.5 copy-start
  7.2 58.0 %all-gather.7.cloned.1.call-start = ((), (), s32[]{:S(2)}) async-start(), calls=%async_computation.4 | async-start | bytes 5242880 | tf_op jit(solution)/shard_map/all_gather | solution.py:49
  7.9 139.6 %all-gather.5.cloned.1.call-start = ((), (), s32[]{:S(2)}) async-start(), calls=%async_computation.3 | async-start | bytes 5242880 | tf_op jit(solution)/shard_map/all_gather | solution.py:48
  8.7 154.0 %reduce-scatter.2.cloned.1.call-start = ((), (), s32[]{:S(2)}) async-start(), calls=%async_computation.2 | async-start | bytes 786432 | tf_op jit(solution)/shard_map/reduce_scatter | solution.py:58
  8.7 160.6 %collective-permute-start = (bf16[2,64,1,4096]{3,1,2,0:T(8,128)(2,1)S(1)}, bf16[2,64,1,4096]{3,1,2,0:T(8,128)(2,1)}, u32[]{:S(2)}, u32[]{:S(2)}) collective-permute-start(bf16[2,64,1,4096]{3,1,2,0:T(8,128)(2,1)S(1)} %copy-done), channel_id=1, source_target_pairs={{0,1},{1,0},{2,3},{3,2},{4,5},{5,4},{6,7},{7,6},{8,9},{9,8},{10,11... | collective-permute-start | bytes 3145736 | tf_op jit(solution)/shard_map/ppermute | solution.py:15
  9.3 160.1 %collective-permute-start.1 = (bf16[2,64,1,4096]{3,1,2,0:T(8,128)(2,1)S(1)}, bf16[2,64,1,4096]{3,1,2,0:T(8,128)(2,1)}, u32[]{:S(2)}, u32[]{:S(2)}) collective-permute-start(bf16[2,64,1,4096]{3,1,2,0:T(8,128)(2,1)S(1)} %copy-done), channel_id=1, source_target_pairs={{1,0},{0,1},{3,2},{2,3},{5,4},{4,5},{7,6},{6,7},{9,8},{8,9},{11,10... | collective-permute-start | bytes 3145736 | tf_op jit(solution)/shard_map/ppermute | solution.py:18
  147.5 3.4 %copy-start.2 = (bf16[2,256,1,4096]{3,1,2,0:T(8,128)(2,1)S(1)}, bf16[2,256,1,4096]{3,1,2,0:T(8,128)(2,1)}, u32[]{:S(2)}) copy-start(bf16[2,256,1,4096]{3,1,2,0:T(8,128)(2,1)} %all-gather.7.cloned.1.call-done) | copy-start | bytes 12582916
  150.9 2.8 %copy-start.3 = (bf16[2,256,1,4096]{3,1,2,0:T(8,128)(2,1)S(1)}, bf16[2,256,1,4096]{3,1,2,0:T(8,128)(2,1)}, u32[]{:S(2)}) copy-start(bf16[2,256,1,4096]{3,1,2,0:T(8,128)(2,1)} %all-gather.5.cloned.1.call-done) | copy-start | bytes 12582916
  156.7 12.6 %copy-start.1 = (f32[1,4096]{1,0:T(1,128)S(1)}, f32[1,4096]{1,0:T(1,128)}, u32[]{:S(2)}) copy-start(f32[1,4096]{1,0:T(1,128)} %param.3) | copy-start | bytes 49156
  164.5 14.2 %all-to-all-start = ((f32[128,2,256]{0,1,2:T(2,128)}), f32[128,2,256]{0,1,2:T(2,128)S(1)}, u32[]{:S(2)}, u32[]{:S(2)}) async-start(f32[128,2,256]{0,1,2:T(2,128)} %copy.7), calls=%async_computation.1 | async-start | bytes 524288 | tf_op jit(solution)/shard_map/all_to_all | solution.py:62
Sparse Core Ops, SparseCore 0:
  9.8 55.2 all-gather.6
  66.7 80.7 all-gather.4
  156.2 6.3 reduce-scatter.1
where the time goes:
time: 186 us
  waiting for transfers between devices  140 us (75%)
  between operations  13.8 us (7%)
  local copies, waits for them, and re-layouts  11.5 us (6%)
  other arithmetic  8.25 us (4%)
  matrix products  7.07 us (4%)
  starting transfers between devices  5.54 us (3%)
    all_gather x1, waiting for transfers between devices, shards(): panel = lax.all_gather(flat, 'col', axis=1, tiled=True)  82.3 us
    all_gather x1, waiting for transfers between devices, shards(): other = lax.all_gather(flat, 'row', axis=1, tiled=True)  50.1 us
    dot_general x4, matrix products, contract(): lax.dot_general(left, right, (((1,), (1,)), ((), ())), preferred_element_...  7.07 us
    convert_element_type x1, other arithmetic, apply_operator(): return (-0.5 * lap + potential[None, None] * center).astype(jnp.bfloat16)  6.81 us
    all_to_all x1, starting transfers between devices, shards(): lax.all_to_all(intersection, 'col', split_axis=2, concat_axis=2, tiled=True)  4.79 us
  transfers between devices with their start and end apart: 6, of which 4 were waited for; matrix products, arithmetic and copies ran while one was open for 14% of the time, Pallas kernels for 0%

commit v1 on v0

--- a/solution.py
+++ b/solution.py
@@ -46,7 +46,12 @@
     parts, orbs, planes, cells = orbitals.shape
     flat = orbitals.reshape(parts, orbs, planes * cells)
     panel = lax.all_gather(flat, "col", axis=1, tiled=True)
-    other = lax.all_gather(flat, "row", axis=1, tiled=True)
+    ring = [flat]
+    for hop in range(3):
+        ring.append(lax.ppermute(ring[-1], "row", [(dev, (dev + 1) % 4) for dev in range(4)]))
+    other = jnp.roll(
+        jnp.concatenate(ring[::-1], axis=1), (lax.axis_index("row") + 1) * ring[0].shape[1], axis=1
+    )
     padded = with_halo(orbitals, (("depth", 2),), 1)
     applied = apply_operator(padded, potential)
     dvol = 1.0 / (planes * lax.axis_size("depth") * cells)

time: 186 us -> 144 us (0.77)
  waiting for transfers between devices: 140 us -> 75 us
  local copies, waits for them, and re-layouts: 11.5 us -> 27.2 us
  starting transfers between devices: 5.54 us -> 9.28 us
  matrix products: 7.07 us -> 10.1 us
    all_gather x1, waiting for transfers between devices: 82.3 us -> 0.01 us  [shards(): panel = lax.all_gather(flat, 'col', axis=1, tiled=True)]
    ppermute x0 -> x3, waiting for transfers between devices: none -> 67.4 us  [shards(): lax.ppermute(ring[-1], 'row', [(dev, (dev + 1) % 4) for dev in range(4)])]
    all_gather x1 -> x0, waiting for transfers between devices: 50.1 us -> none  [shards(): other = lax.all_gather(flat, 'row', axis=1, tiled=True)]
    unnamed x9 -> x14, local copies, waits for them, and re-layouts: 1.52 us -> 15.9 us
    ppermute x0 -> x3, starting transfers between devices: none -> 3.8 us  [shards(): lax.ppermute(ring[-1], 'row', [(dev, (dev + 1) % 4) for dev in range(4)])]
    dot_general x4, matrix products: 7.07 us -> 10.1 us  [contract(): lax.dot_general(left, right, (((1,), (1,)), ((), ())), preferred_element_...]
  transfers between devices with their start and end apart: 6 -> 8, of which waited for: 4 -> 5; matrix products, arithmetic and copies ran while one was open for 14% -> 31% of each run, Pallas kernels for 0% -> 0%
where the time goes in v1:
time: 144 us
  waiting for transfers between devices  75 us (52%)
  local copies, waits for them, and re-layouts  27.2 us (19%)
  between operations  14.1 us (10%)
  matrix products  10.1 us (7%)
  starting transfers between devices  9.28 us (6%)
  other arithmetic  8.25 us (6%)
    ppermute x3, waiting for transfers between devices, shards(): lax.ppermute(ring[-1], 'row', [(dev, (dev + 1) % 4) for dev in range(4)])  67.4 us
    unnamed x14, local copies, waits for them, and re-layouts  15.9 us
    dot_general x4, matrix products, contract(): lax.dot_general(left, right, (((1,), (1,)), ((), ())), preferred_element_...  10.1 us
    convert_element_type x1, other arithmetic, apply_operator(): return (-0.5 * lap + potential[None, None] * center).astype(jnp.bfloat16)  6.81 us
    reduce_scatter x1, waiting for transfers between devices, shards(): lax.psum_scatter(dvol * jnp.concatenate([sreal, simag], axis=1), 'depth',...  4.99 us
    all_to_all x1, starting transfers between devices, shards(): lax.all_to_all(intersection, 'col', split_axis=2, concat_axis=2, tiled=True)  4.83 us
    ppermute x3, starting transfers between devices, shards(): lax.ppermute(ring[-1], 'row', [(dev, (dev + 1) % 4) for dev in range(4)])  3.8 us
    slice x2, local copies, waits for them, and re-layouts, apply_operator(): yplus = jnp.roll(center, -NX, axis=3)  3.18 us
  transfers between devices with their start and end apart: 8, of which 5 were waited for; matrix products, arithmetic and copies ran while one was open for 31% of the time, Pallas kernels for 0%

profile of v1, /device:TPU:0, one launch (start us, length us, event | category | flops | bytes accessed | tf_op | source)
XLA Modules:
  0.0 143.9 jit_solution(1244582738047880500)
XLA Ops:
  7.2 0.0 copy-start
  7.2 0.0 all-gather.3.cloned.1.call-start
  7.2 3.0 %collective-permute-start = (bf16[2,64,4096]{2,1,0:T(8,128)(2,1)}, bf16[2,64,4096]{2,1,0:T(8,128)(2,1)}, u32[]{:S(2)}, u32[]{:S(2)}) collective-permute-start(bf16[2,64,4096]{2,1,0:T(8,128)(2,1)} %bitcast.41), channel_id=1, source_target_pairs={{0,8},{8,16},{16,24},{24,0},{1,9},{9,17},{17,25},{25,1},{2,10},{10... | collective-permute-start | bytes 3145736 | tf_op jit(solution)/shard_map/ppermute | solution.py:51
  10.2 0.0 all-gather.3.cloned.1.call-update
  10.3 0.0 reduce-scatter.2.cloned.1.call-start
  10.3 0.1 collective-permute-start.3
  10.4 0.5 collective-permute-start.4
  10.9 23.8 %collective-permute-done = bf16[2,64,4096]{2,1,0:T(8,128)(2,1)} collective-permute-done((bf16[2,64,4096]{2,1,0:T(8,128)(2,1)}, bf16[2,64,4096]{2,1,0:T(8,128)(2,1)}, u32[]{:S(2)}, u32[]{:S(2)}) %collective-permute-start) | collective-permute-done | bytes 1048608 | tf_op jit(solution)/shard_map/ppermute | solution.py:51
  34.7 0.8 collective-permute-start.1
  35.5 0.0 copy-done
  35.5 1.8 %fusion.27 = (f32[2,64,1,4033]{3,1,2,0:T(8,128)S(1)}, f32[2,64,1,4033]{3,1,2,0:T(8,128)}) fusion(bf16[2,64,1,4096]{3,1,2,0:T(8,128)(2,1)S(1)} %copy-done), kind=kLoop, calls=%fused_computation.45 | loop fusion | bytes 8259584 | tf_op jit(solution)/shard_map/jit(_roll_static)/slice | solution.py:33
  37.3 0.1 fusion.26
  37.4 0.7 fusion.29
  38.1 22.1 %collective-permute-done.1 = bf16[2,64,4096]{2,1,0:T(8,128)(2,1)} collective-permute-done((bf16[2,64,4096]{2,1,0:T(8,128)(2,1)}, bf16[2,64,4096]{2,1,0:T(8,128)(2,1)}, u32[]{:S(2)}, u32[]{:S(2)}) %collective-permute-start.1) | collective-permute-done | bytes 1048608 | tf_op jit(solution)/shard_map/ppermute | solution.py:51
  60.2 0.0 collective-permute-start.2
  60.2 0.7 fusion.25
  60.9 2.5 %fusion.28 = (f32[2,64,1,4032]{3,1,2,0:T(8,128)}, f32[2,64,1,4032]{3,1,2,0:T(8,128)}) fusion(bf16[2,64,1,4096]{3,1,2,0:T(8,128)(2,1)S(1)} %copy-done), kind=kLoop, calls=%fused_computation.46 | loop fusion | bytes 8257536 | tf_op jit(solution)/shard_map/jit(_roll_static)/slice | solution.py:30
  63.4 21.5 %collective-permute-done.2 = bf16[2,64,4096]{2,1,0:T(8,128)(2,1)} collective-permute-done((bf16[2,64,4096]{2,1,0:T(8,128)(2,1)}, bf16[2,64,4096]{2,1,0:T(8,128)(2,1)}, u32[]{:S(2)}, u32[]{:S(2)}) %collective-permute-start.2) | collective-permute-done | bytes 1048608 | tf_op jit(solution)/shard_map/ppermute | solution.py:51
  84.9 2.3 %constant_dynamic-update-slice_fusion.7 = bf16[2,512,4096]{2,1,0:T(8,128)(2,1)} fusion(bf16[2,64,4096]{2,1,0:T(8,128)(2,1)} %collective-permute-done.2), kind=kLoop, calls=%fused_computation.31 | loop fusion | bytes 2097152
  87.2 2.3 %constant_dynamic-update-slice_fusion.6 = bf16[2,512,4096]{2,1,0:T(8,128)(2,1)} fusion(bf16[2,512,4096]{2,1,0:T(8,128)(2,1)} %constant_dynamic-update-slice_fusion.7, bf16[2,64,4096]{2,1,0:T(8,128)(2,1)} %collective-permute-done.1), kind=kLoop, calls=%fused_computation.30 | loop fusion | bytes 2097152
  89.5 2.3 %constant_dynamic-update-slice_fusion.5 = bf16[2,512,4096]{2,1,0:T(8,128)(2,1)} fusion(bf16[2,512,4096]{2,1,0:T(8,128)(2,1)} %constant_dynamic-update-slice_fusion.6, bf16[2,64,4096]{2,1,0:T(8,128)(2,1)} %collective-permute-done), kind=kLoop, calls=%fused_computation.29 | loop fusion | bytes 2097152
  91.7 1.1 constant_dynamic-update-slice_fusion.4
  92.8 2.3 %constant_dynamic-update-slice_fusion.3 = bf16[2,512,4096]{2,1,0:T(8,128)(2,1)} fusion(bf16[2,512,4096]{2,1,0:T(8,128)(2,1)} %constant_dynamic-update-slice_fusion.4, bf16[2,64,4096]{2,1,0:T(8,128)(2,1)} %collective-permute-done.2), kind=kLoop, calls=%fused_computation.27 | loop fusion | bytes 2097152
  95.1 2.3 %constant_dynamic-update-slice_fusion.2 = bf16[2,512,4096]{2,1,0:T(8,128)(2,1)} fusion(bf16[2,512,4096]{2,1,0:T(8,128)(2,1)} %constant_dynamic-update-slice_fusion.3, bf16[2,64,4096]{2,1,0:T(8,128)(2,1)} %collective-permute-done.1), kind=kLoop, calls=%fused_computation.26 | loop fusion | bytes 2097152
  97.4 2.3 %constant_dynamic-update-slice_fusion.1 = bf16[2,512,4096]{2,1,0:T(8,128)(2,1)} fusion(bf16[2,512,4096]{2,1,0:T(8,128)(2,1)} %constant_dynamic-update-slice_fusion.2, bf16[2,64,4096]{2,1,0:T(8,128)(2,1)} %collective-permute-done), kind=kLoop, calls=%fused_computation.25 | loop fusion | bytes 2097152
  99.7 1.1 constant_dynamic-update-slice_fusion
  100.8 0.0 all-gather.3.cloned.1.call-done
  100.8 0.0 copy-start.2
  100.8 3.1 %fusion.9 = f32[256,256]{1,0:T(8,128)S(1)} fusion(bf16[2,256,1,4096]{3,1,2,0:T(8,128)(2,1)} %all-gather.3.cloned.1.call-done, bf16[2,512,4096]{2,1,0:T(8,128)(2,1)} %constant_dynamic-update-slice_fusion, s32[]{:T(128)S(6)} %select_n.45), kind=kOutput, calls=%fused_computation.16 | convolution fusion | flops 536870912 | bytes 4456452 | tf_op jit(solution)/shard_map/dot_general | solution.py:40
  103.9 0.3 copy-done.2
  104.2 2.3 %fusion.10 = f32[256,256]{1,0:T(8,128)S(1)} fusion(bf16[2,256,1,4096]{3,1,2,0:T(8,128)(2,1)S(1)} %copy-done.2, bf16[2,512,4096]{2,1,0:T(8,128)(2,1)} %constant_dynamic-update-slice_fusion, s32[]{:T(128)S(6)} %add.59, s32[]{:T(128)S(6)} %select_n.45), kind=kOutput, calls=%fused_computation.17 | convolution fusion | flops 536870912 | bytes 4456456 | tf_op jit(solution)/shard_map/dot_general | solution.py:40
  106.6 2.3 %fusion.12 = f32[256,256]{0,1:T(8,128)S(1)} fusion(f32[256,256]{1,0:T(8,128)S(1)} %fusion.10, bf16[2,256,1,4096]{3,1,2,0:T(8,128)(2,1)S(1)} %copy-done.2, bf16[2,512,4096]{2,1,0:T(8,128)(2,1)} %constant_dynamic-update-slice_fusion, s32[]{:T(128)S(6)} %select_n.45), kind=kOutput, calls=%fused_computation.19 | convolution fusion | flops 536936448 | bytes 4718596 | tf_op jit(solution)/shard_map/dot_general | solution.py:40
  108.9 2.3 %fusion.14 = f32[256,256]{0,1:T(8,128)S(1)} fusion(f32[256,256]{1,0:T(8,128)S(1)} %fusion.9, bf16[2,256,1,4096]{3,1,2,0:T(8,128)(2,1)S(1)} %copy-done.2, bf16[2,512,4096]{2,1,0:T(8,128)(2,1)} %constant_dynamic-update-slice_fusion, s32[]{:T(128)S(6)} %add.59, s32[]{:T(128)S(6)} %select_n.45), kind=kOutput, calls=%fused_computation.21 | convolution fusion | flops 536936448 | bytes 4718600 | tf_op jit(solution)/shard_map/dot_general | solution.py:40
  111.3 0.8 maximum_multiply_fusion
  112.1 0.0 reduce-scatter.2.cloned.1.call-update
  112.1 0.6 fusion.17
  112.7 0.0 copy-start.1
  112.7 2.4 %fusion.24 = (f32[2,64,1,4095]{3,1,2,0:T(8,128)}, f32[2,64,1,4095]{3,1,2,0:T(8,128)}) fusion(bf16[2,64,1,4096]{3,1,2,0:T(8,128)(2,1)S(1)} %copy-done), kind=kLoop, calls=%fused_computation.42 | loop fusion | bytes 8386560 | tf_op jit(solution)/shard_map/jit(_roll_static)/slice | solution.py:33
  115.2 5.0 %reduce-scatter.2.cloned.1.call-done = f32[128,512]{0,1:T(8,128)} async-done(((f32[256,512]{0,1:T(8,128)}), f32[128,512]{0,1:T(8,128)}) %reduce-scatter.2.cloned.1.call-update) | async-done | bytes 262160 | tf_op jit(solution)/shard_map/reduce_scatter | solution.py:63
  120.2 1.9 %copy.7 = f32[128,2,256]{0,1,2:T(2,128)} copy(f32[128,2,256]{0,2,1:T(8,128)} %bitcast.42) | data formatting | bytes 524288 | tf_op jit(solution)/shard_map/reshape | solution.py:66
  122.0 4.8 %all-to-all-start = ((f32[128,2,256]{0,1,2:T(2,128)}), f32[128,2,256]{0,1,2:T(2,128)S(1)}, u32[]{:S(2)}, u32[]{:S(2)}) async-start(f32[128,2,256]{0,1,2:T(2,128)} %copy.7), calls=%async_computation.1 | async-start | bytes 524288 | tf_op jit(solution)/shard_map/all_to_all | solution.py:67
  126.8 0.0 collective-permute-done.3
  126.8 0.0 collective-permute-done.4
  126.9 0.0 copy-done.1
  126.9 6.8 %fusion.6 = bf16[2,64,1,4096]{3,1,2,0:T(8,128)(2,1)} fusion(f32[2,64,1,4032]{3,1,2,0:T(8,128)} %get-tuple-element.15, f32[2,64,1,64]{3,1,2,0:T(8,128)} %get-tuple-element.17, f32[2,64,1,64]{3,1,2,0:T(8,128)} %get-tuple-element.16, f32[2,64,1,4032]{3,1,2,0:T(8,128)} %get-tuple-element.14, f32[2,64,1,63]{3,1,2,0:T(8,128)S(1)} %get-tuple-element.11, ...), kind=kLoop, calls=%fused_computation.11 | loop fusion | flops 11534336 | bytes 16801792 | tf_op jit(solution)/shard_map/convert_element_type | solution.py:36
  133.7 2.6 %all-to-all-done = f32[128,2,256]{0,1,2:T(2,128)S(1)} async-done(((f32[128,2,256]{0,1,2:T(2,128)}), f32[128,2,256]{0,1,2:T(2,128)S(1)}, u32[]{:S(2)}, u32[]{:S(2)}) %all-to-all-start) | async-done | bytes 262176 | tf_op jit(solution)/shard_map/all_to_all | solution.py:67
  136.2 0.8 copy.8
Async XLA Ops:
  7.2 28.3 %copy-start = (bf16[2,64,1,4096]{3,1,2,0:T(8,128)(2,1)S(1)}, bf16[2,64,1,4096]{3,1,2,0:T(8,128)(2,1)}, u32[]{:S(2)}) copy-start(bf16[2,64,1,4096]{3,1,2,0:T(8,128)(2,1)} %param.2) | copy-start | bytes 3145732
  7.2 93.6 %all-gather.3.cloned.1.call-start = ((), (), s32[]{:S(2)}) async-start(), calls=%async_computation.3 | async-start | bytes 5242880 | tf_op jit(solution)/shard_map/all_gather | solution.py:48
  7.2 27.5 %collective-permute-start = (bf16[2,64,4096]{2,1,0:T(8,128)(2,1)}, bf16[2,64,4096]{2,1,0:T(8,128)(2,1)}, u32[]{:S(2)}, u32[]{:S(2)}) collective-permute-start(bf16[2,64,4096]{2,1,0:T(8,128)(2,1)} %bitcast.41), channel_id=1, source_target_pairs={{0,8},{8,16},{16,24},{24,0},{1,9},{9,17},{17,25},{25,1},{2,10},{10... | collective-permute-start | bytes 3145736 | tf_op jit(solution)/shard_map/ppermute | solution.py:51
  10.3 109.9 %reduce-scatter.2.cloned.1.call-start = ((), (), s32[]{:S(2)}) async-start(), calls=%async_computation.2 | async-start | bytes 786432 | tf_op jit(solution)/shard_map/reduce_scatter | solution.py:63
  10.3 116.5 %collective-permute-start.3 = (bf16[2,64,1,4096]{3,1,2,0:T(8,128)(2,1)}, bf16[2,64,1,4096]{3,1,2,0:T(8,128)(2,1)}, u32[]{:S(2)}, u32[]{:S(2)}) collective-permute-start(bf16[2,64,1,4096]{3,1,2,0:T(8,128)(2,1)} %param.2), channel_id=1, source_target_pairs={{0,1},{1,0},{2,3},{3,2},{4,5},{5,4},{6,7},{7,6},{8,9},{9,8},{10,11... | collective-permute-start | bytes 3145736 | tf_op jit(solution)/shard_map/ppermute | solution.py:15
  10.4 116.5 %collective-permute-start.4 = (bf16[2,64,1,4096]{3,1,2,0:T(8,128)(2,1)}, bf16[2,64,1,4096]{3,1,2,0:T(8,128)(2,1)}, u32[]{:S(2)}, u32[]{:S(2)}) collective-permute-start(bf16[2,64,1,4096]{3,1,2,0:T(8,128)(2,1)} %param.2), channel_id=1, source_target_pairs={{1,0},{0,1},{3,2},{2,3},{5,4},{4,5},{7,6},{6,7},{9,8},{8,9},{11,10... | collective-permute-start | bytes 3145736 | tf_op jit(solution)/shard_map/ppermute | solution.py:18
  34.7 25.5 %collective-permute-start.1 = (bf16[2,64,4096]{2,1,0:T(8,128)(2,1)}, bf16[2,64,4096]{2,1,0:T(8,128)(2,1)}, u32[]{:S(2)}, u32[]{:S(2)}) collective-permute-start(bf16[2,64,4096]{2,1,0:T(8,128)(2,1)} %collective-permute-done), channel_id=1, source_target_pairs={{0,8},{8,16},{16,24},{24,0},{1,9},{9,17},{17,25},{25,1},{2,10},{10... | collective-permute-start | bytes 3145736 | tf_op jit(solution)/shard_map/ppermute | solution.py:51
  60.2 24.7 %collective-permute-start.2 = (bf16[2,64,4096]{2,1,0:T(8,128)(2,1)}, bf16[2,64,4096]{2,1,0:T(8,128)(2,1)}, u32[]{:S(2)}, u32[]{:S(2)}) collective-permute-start(bf16[2,64,4096]{2,1,0:T(8,128)(2,1)} %collective-permute-done.1), channel_id=1, source_target_pairs={{0,8},{8,16},{16,24},{24,0},{1,9},{9,17},{17,25},{25,1},{2,10},{10... | collective-permute-start | bytes 3145736 | tf_op jit(solution)/shard_map/ppermute | solution.py:51
  100.8 3.4 %copy-start.2 = (bf16[2,256,1,4096]{3,1,2,0:T(8,128)(2,1)S(1)}, bf16[2,256,1,4096]{3,1,2,0:T(8,128)(2,1)}, u32[]{:S(2)}) copy-start(bf16[2,256,1,4096]{3,1,2,0:T(8,128)(2,1)} %all-gather.3.cloned.1.call-done) | copy-start | bytes 12582916
  112.7 14.1 %copy-start.1 = (f32[1,4096]{1,0:T(1,128)S(1)}, f32[1,4096]{1,0:T(1,128)}, u32[]{:S(2)}) copy-start(f32[1,4096]{1,0:T(1,128)} %param.3) | copy-start | bytes 49156
  122.0 14.2 %all-to-all-start = ((f32[128,2,256]{0,1,2:T(2,128)}), f32[128,2,256]{0,1,2:T(2,128)S(1)}, u32[]{:S(2)}, u32[]{:S(2)}) async-start(f32[128,2,256]{0,1,2:T(2,128)} %copy.7), calls=%async_computation.1 | async-start | bytes 524288 | tf_op jit(solution)/shard_map/all_to_all | solution.py:67
Sparse Core Ops, SparseCore 0:
  10.4 82.6 all-gather.2
  112.3 7.8 reduce-scatter.1
